TPU v7x, 512 devices: a whole 4x4x16 slice. The times are simulated.
512 devices in a mesh: date: 64 (over z, y), prod: 8 (over x, core).
Axes of the slice: x: 4, y: 4, z: 16, core: 2. Of those that a mesh axis runs over, the one named last changes fastest.
Arguments:
- daily_sales: float32 [256, 2048, 128], P('prod', 'date'), may hold values from -2.5 to 2.5
- week_id: int32 [2048], P('date'), may hold values from 0 to 409, never falling along the last dimension, each value on 1 to 7 neighbouring positions
- month_id: int32 [2048], P('date'), may hold values from 0 to 85, never falling along the last dimension, each value on 1 to 31 neighbouring positions
- year_id: int32 [2048], P('date'), may hold values from 0 to 6, never falling along the last dimension, each value on 1 to 366 neighbouring positions
Outputs:
- running: float32 [256, 2048, 128], P('prod', 'date')
- week_total: float32 [256, 2048, 128], P('prod', 'date')
- month_total: float32 [256, 2048, 128], P('prod', 'date')
- year_total: float32 [256, 2048, 128], P('prod', 'date')
- store_rollup: float32 [4, 2048, 128], P(None, 'date')
Inputs may be any that keep to these rules, and one draw needn't show every extreme that they name: `week_id`: starts at 0 and never falls along the dates; each week covers 1 to 7 consecutive dates and some cover exactly 7. `month_id`: starts at 0 and never falls along the dates; each month covers 1 to 31 consecutive dates and some cover exactly 31; months need not line up with weeks. `year_id`: starts at 0 and never falls along the dates; each year covers 1 to 366 consecutive dates and some cover exactly 366; years need not line up with weeks or months.
All inputs are finite; a program needn't handle non-finite values.
Results may differ from a plain program's by a relative error of at most 0.000094.
Values sent between devices are 32-bit elements.
A program may use at most 64 MiB of HBM per device.

v0:
```python
import jax
import jax.numpy as jnp
from jax import lax
from jax.sharding import Mesh
from jax.sharding import PartitionSpec as P

DATE = ("date_0", "date_1")


far_index = 1 << 30


def nothing_yet(array, identity):
    return jax.tree.map(
        lambda a, e: jnp.broadcast_to(jnp.asarray(e, a.dtype), a.shape), array, identity
    )


def carried_in(array, axes, combine, identity, reverse):
    before = start = nothing_yet(array, identity)
    running = array
    for axis in reversed(axes):
        length, place = (lax.axis_size(axis), lax.axis_index(axis))
        pieces = jax.tree.map(lambda part: lax.all_gather(part, axis), running)
        inside, running = (start, start)
        for k in reversed(range(length)) if reverse else range(length):
            passed = k > place if reverse else k < place
            running = combine(running, jax.tree.map(lambda part: part[k], pieces))
            inside = jax.tree.map(lambda new, old: jnp.where(passed, new, old), running, inside)
        before = combine(inside, before)
    return before


def total_of_pieces(array, axis):
    blocks = lax.all_gather(array, axis)
    return blocks.sum(axis=0)


def forward(earlier, latter):
    top_early, sums_early = earlier
    top_later, sums_later = latter
    inside = (top_later <= top_early)[:, None, None]
    return (jnp.maximum(top_early, top_later), sums_later + jnp.where(inside, sums_early, 0.0))


def backward(earlier, latter):
    low_early, sums_early = earlier
    low_later, sums_later = latter
    inside = (low_later >= low_early)[:, None, None]
    return (jnp.minimum(low_early, low_later), sums_later + jnp.where(inside, sums_early, 0.0))


def match_keep(ids_seen, ids_own, partial_value):
    return jnp.where((ids_seen == ids_own)[:, None, None], partial_value, 0.0)


def local(daily_sales, week_id, month_id, year_id):
    columns = daily_sales.shape[0]
    span_len = daily_sales.shape[1]
    level_ids = jnp.stack([jnp.zeros_like(week_id), week_id, month_id, year_id])
    offsets = lax.iota(jnp.int32, span_len)
    lower = (offsets[None, :] <= offsets[:, None]).astype(jnp.float32)
    matches = (level_ids[1:, :, None] == level_ids[1:, None, :]).astype(jnp.float32)
    mixers = jnp.concatenate([lower[None], matches], axis=0)
    within = jnp.einsum("kij,pjs->kpis", mixers, daily_sales, precision=lax.Precision.HIGHEST)
    tail_sums = within[:, :, -1, :]
    head_sums = within[1:, :, 0, :]
    first_ids = level_ids[:, 0]
    last_ids = level_ids[:, -1]
    start = (jnp.full((4,), -1, jnp.int32), jnp.zeros_like(tail_sums))
    top_prev, sums_prev = carried_in((last_ids, tail_sums), DATE, forward, start, False)
    carry_in = match_keep(top_prev, first_ids, sums_prev)
    finish = (jnp.full((3,), far_index, jnp.int32), jnp.zeros_like(head_sums))
    low_next, sums_next = carried_in((first_ids[1:], head_sums), DATE, backward, finish, True)
    carry_back = match_keep(low_next, last_ids[1:], sums_next)
    start_gain = (level_ids[1:] == first_ids[1:, None]).astype(jnp.float32)
    end_gain = (level_ids[1:] == last_ids[1:, None]).astype(jnp.float32)
    running = within[0] + carry_in[0][:, None, :]
    levels = (
        within[1:]
        + carry_in[1:, :, None, :] * start_gain[:, None, :, None]
        + carry_back[:, :, None, :] * end_gain[:, None, :, None]
    )
    product_terms = jnp.concatenate(
        [jnp.sum(running, axis=0)[None], jnp.sum(levels, axis=1)], axis=0
    )
    store_rollup = total_of_pieces(product_terms, "prod")
    return (running, levels[0, :columns], levels[1, :columns], levels[2, :columns], store_rollup)


def solution(mesh):
    finer = Mesh(mesh.devices.reshape(16, 4, mesh.shape["prod"]), ("date_0", "date_1", "prod"))
    return jax.shard_map(
        local,
        mesh=finer,
        in_specs=(P("prod", DATE, None), P(DATE), P(DATE), P(DATE)),
        out_specs=(
            P("prod", DATE, None),
            P("prod", DATE, None),
            P("prod", DATE, None),
            P("prod", DATE, None),
            P(None, DATE, None),
        ),
        check_vma=False,
    )
```

profile of v0, /device:TPU:1, one launch (start us, length us, event | category | flops | bytes accessed | tf_op | source)
XLA Modules:
  0.0 168.6 jit_solution(11447396755380277915)
XLA Ops:
  7.2 0.7 pad_add_fusion
  8.0 0.2 slice_reduce_fusion.1
  8.2 0.1 broadcast_compare_fusion
  8.3 0.8 pad_add_fusion.1
  9.0 0.2 slice_reduce_fusion.2
  9.2 1.3 dynamic-slice
  11.8 0.2 dynamic-update-slice.1
  12.0 0.2 dynamic-update-slice
  12.2 7.8 %all-reduce.2 = (s32[16]{0:T(128)S(1)}, s32[12]{0:T(128)S(1)}) all-reduce(s32[16]{0:T(128)S(1)} %dynamic-update-slice, s32[12]{0:T(128)S(1)} %dynamic-update-slice.1), channel_id=2, replica_groups=mesh['date_0'=16,'date_1'=4,'prod'=8] {'date_1'}, use_global_device_ids=true, to_apply=%add | all-reduce | flops 28 | bytes 224
  20.1 0.1 fusion.94
  20.2 0.1 slice_compare_fusion.2
  20.3 0.1 compare_bitcast_fusion.9
  20.4 1.0 convolution_bitcast_fusion
  21.4 9.4 %all-gather.1 = f32[16,32,1,128]{3,1,2,0:T(8,128)S(1)} all-gather(f32[4,32,1,128]{3,1,2,0:T(8,128)S(1)} %bitcast.764), channel_id=3, replica_groups=mesh['date_0'=16,'date_1'=4,'prod'=8] {'date_1'}, dimensions={0}, use_global_device_ids=true | all-gather | bytes 327680 | tf_op jit(solution)/shard_map/all_gather | solution.py:24
  30.8 0.7 fusion.26
  31.5 0.1 fusion.95
  31.6 0.1 slice_compare_fusion
  31.7 0.1 compare_bitcast_fusion.7
  31.9 29.0 %all-gather.6 = s32[16,1,3]{2,1,0:T(1,128)S(1)} all-gather(s32[1,1,3]{2,1,0:T(1,128)S(1)} %get-tuple-element.25), channel_id=1, replica_groups=mesh['date_0'=16,'date_1'=4,'prod'=8] {'date_0'}, dimensions={0}, use_global_device_ids=true | all-gather | bytes 204 | tf_op jit(solution)/shard_map/all_gather | solution.py:24
  60.9 0.1 fusion.67
  61.1 19.3 %all-gather.5 = s32[16,1,4]{2,1,0:T(1,128)S(1)} all-gather(s32[1,1,4]{2,1,0:T(1,128)S(1)} %get-tuple-element.37), channel_id=1, replica_groups=mesh['date_0'=16,'date_1'=4,'prod'=8] {'date_0'}, dimensions={0}, use_global_device_ids=true | all-gather | bytes 272 | tf_op jit(solution)/shard_map/all_gather | solution.py:24
  80.4 0.1 fusion.68
  80.5 9.6 %all-gather.3 = f32[12,32,1,128]{3,1,2,0:T(8,128)S(1)} all-gather(f32[3,32,1,128]{3,1,2,0:T(8,128)S(1)} %bitcast.765), channel_id=5, replica_groups=mesh['date_0'=16,'date_1'=4,'prod'=8] {'date_1'}, dimensions={0}, use_global_device_ids=true | all-gather | bytes 245760 | tf_op jit(solution)/shard_map/all_gather | solution.py:24
  90.3 0.1 fusion.57
  90.4 26.6 %all_gather.45 = f32[16,3,32,128]{3,2,1,0:T(8,128)S(1)} all-gather(f32[1,3,32,128]{3,2,1,0:T(8,128)S(1)} %fusion.57), channel_id=1, replica_groups=mesh['date_0'=16,'date_1'=4,'prod'=8] {'date_0'}, dimensions={0}, use_global_device_ids=true | all-gather | bytes 835584 | tf_op jit(solution)/shard_map/all_gather | solution.py:24
  117.0 0.2 fusion.52
  117.2 1.5 fusion.21
  118.8 0.9 fusion.96
  119.7 0.4 fusion.98
  120.0 39.9 %all-gather.4 = f32[32,32,128]{2,1,0:T(8,128)S(1)} all-gather(f32[4,32,128]{2,1,0:T(8,128)S(1)} %pad_maximum_fusion), channel_id=6, replica_groups=mesh['date_0'=16,'date_1'=4,'prod'=8] {'prod'}, dimensions={0}, use_global_device_ids=true | all-gather | bytes 589824 | tf_op jit(solution)/shard_map/all_gather | solution.py:35
  159.9 1.2 slice_bitcast_fusion
  161.1 0.7 reduce_sum.29
  (32 shorter events, 0.4 us)
Async XLA Ops:
  7.2 13.2 %copy-start = (f32[32,32,128]{2,1,0:T(8,128)S(1)}, f32[32,32,128]{2,1,0:T(8,128)}, u32[]{:S(2)}) copy-start(f32[32,32,128]{2,1,0:T(8,128)} %param.4) | copy-start | bytes 1572868
  7.2 110.1 %all-gather.9.cloned.1.call-start = ((), (), s32[]{:S(2)}) async-start(), calls=%async_computation | async-start | bytes 1114112 | tf_op jit(solution)/shard_map/all_gather | solution.py:24
  20.3 69.9 %copy-start.1 = (s32[32]{0:T(128)S(1)}, s32[32]{0:T(128)}, u32[]{:S(2)}) copy-start(s32[32]{0:T(128)} %param.7) | copy-start | bytes 388
  20.3 69.9 %copy-start.2 = (s32[32]{0:T(128)S(1)}, s32[32]{0:T(128)}, u32[]{:S(2)}) copy-start(s32[32]{0:T(128)} %param.6) | copy-start | bytes 388
  20.3 69.9 %copy-start.3 = (s32[32]{0:T(128)S(1)}, s32[32]{0:T(128)}, u32[]{:S(2)}) copy-start(s32[32]{0:T(128)} %param.5) | copy-start | bytes 388
Sparse Core Ops, SparseCore 0:
  31.6 67.9 all-gather.8
where the time goes:
time: 169 us
  blocking collectives  142 us (84%)
  between operations  15.7 us (9%)
  other arithmetic  6.78 us (4%)
  local copies, waits for them, and re-layouts  3.4 us (2%)
    all_gather x5, blocking collectives, carried_in(): pieces = jax.tree.map(lambda part: lax.all_gather(part, axis), running)  94 us
    all_gather x1, blocking collectives, total_of_pieces(): blocks = lax.all_gather(array, axis)  39.9 us
    unnamed x1, blocking collectives  7.85 us
  transfers between devices with their start and end apart: 1, of which 0 were waited for; matrix products, arithmetic and copies ran while one was open for 1% of the time, Pallas kernels for 0%

commit v1 on v0

v1 whole, which is shorter than its diff:
```python
import functools

import jax
import jax.numpy as jnp
from jax import lax
from jax.experimental import pallas as pl
from jax.experimental.pallas import tpu as pltpu
from jax.sharding import PartitionSpec as P

MESH = pl.DeviceIdType.MESH
F32 = jnp.float32
I32 = jnp.int32

NZ, NY, NX, NC = 16, 4, 4, 2
REACH = 4
OFFS = (-4, -3, -2, -1, 1, 2, 3, 4)
SLOT = {o: i for i, o in enumerate(OFFS)}
SPAN = 32
COLS = 32
L = 128

RUN, WIN, MIN, YIN, WBK, MBK, YBK = range(7)


def spread(ids):
    sub = lax.broadcasted_iota(I32, (8, L), 0)
    tiles = []
    for j in range(SPAN // 8):
        v = jnp.full((8, L), ids[8 * j], I32)
        for r in range(1, 8):
            v = jnp.where(sub == r, ids[8 * j + r], v)
        tiles.append(v)
    return jnp.concatenate(tiles, axis=0)


def row_of(scalar):
    return jnp.full((1, L), scalar, I32).astype(F32)


def gate(cond):
    return jnp.where(cond, 1.0, 0.0).astype(F32)


def same(a, b):
    return jnp.where(a == b, 1.0, 0.0).astype(F32)


def stack_rows(rows):
    sub = lax.broadcasted_iota(I32, (8, L), 0)
    out = jnp.zeros((8, L), F32)
    for r, row in enumerate(rows):
        if row is not None:
            out = jnp.where(sub == r, row, out)
    return out


def exchange(
    wk, mo, yr, x_hbm, carry, glob,
    xv, a_out, a_in, w_out, w_in, p_out, p_in, x_in,
    b_out, b_in, b2_out, b2_in, c1_out, c1_in, c2_out, c2_in,
    g_out, g_in, gb_out, gb_in, gb2_out, gb2_in,
    ld_sem, send_sem, a_sem, w_sem, p_sem, x_sem, b_sem, b2_sem, c1_sem, c2_sem,
    g_sem, gb_sem, gb2_sem,
):
    d = lax.axis_index("date")
    pr = lax.axis_index("prod")
    z, y = lax.div(d, NY), lax.rem(d, NY)
    xx, core = lax.div(pr, NC), lax.rem(pr, NC)

    loads = [
        pltpu.make_async_copy(x_hbm.at[pl.ds(8 * q, 8)], xv.at[pl.ds(8 * q, 8)], ld_sem.at[q])
        for q in range(4)
    ]
    for cp in loads:
        cp.start()

    def y_dev(j):
        return z * NY + lax.rem(y + j, NY)

    def z_pos(k):
        return lax.rem(z + k + NZ, NZ)

    def z_dev(k):
        return z_pos(k) * NY + y

    def x_dev(j):
        return lax.rem(xx + j, NX) * NC + core

    after = lax.rem(d + 1, NZ * NY)
    ahead = lax.rem(d + NZ * NY - 1, NZ * NY)
    mate = xx * NC + (1 - core)

    barrier = pltpu.get_barrier_semaphore()
    partners = [(z_dev(k), pr) for k in (4, -4, 3, -3, 2, -2, 1, -1)]
    partners += [(y_dev(j), pr) for j in (2, 1, 3)]
    partners += [(d, x_dev(j)) for j in (2, 1, 3)]
    partners += [(d, mate), (after, pr), (ahead, pr)]
    for dev in partners:
        pl.semaphore_signal(barrier, inc=1, device_id=dev, device_id_type=MESH)

    sends = []

    def send(src, dst, sem, dev):
        cp = pltpu.make_async_remote_copy(
            src_ref=src, dst_ref=dst, send_sem=send_sem.at[len(sends)], recv_sem=sem,
            device_id=dev, device_id_type=MESH,
        )
        cp.start()
        sends.append(cp)

    def landed(ref, sem):
        pltpu.make_async_remote_copy(
            src_ref=ref, dst_ref=ref, send_sem=send_sem.at[0], recv_sem=sem,
            device_id=(d, pr), device_id_type=MESH,
        ).wait_recv()

    wid, mid, yid = spread(wk), spread(mo), spread(yr)
    wf, wl = wk[0], wk[SPAN - 1]
    mf, ml = mo[0], mo[SPAN - 1]
    yf, yl = yr[0], yr[SPAN - 1]
    wt_m, wh_m = gate(wid == wl), gate(wid == wf)
    mt_m, mh_m = gate(mid == ml), gate(mid == mf)
    yt_m, yh_m = gate(yid == yl), gate(yid == yf)
    wf_r, wl_r, mf_r, ml_r, yf_r, yl_r = (row_of(v) for v in (wf, wl, mf, ml, yf, yl))
    y_ids = stack_rows([yf_r, yl_r])

    for q in range(4):
        loads[q].wait()
        v = xv[pl.ds(8 * q, 8)]
        a_out[q, 0:8] = jnp.sum(v, axis=1)
        a_out[q, 8:16] = jnp.sum(v * yt_m[None], axis=1)
        a_out[q, 16:24] = jnp.sum(v * yh_m[None], axis=1)
        a_out[q, 24:32] = y_ids
    p_out[...] = jnp.sum(xv[...], axis=0)

    pl.semaphore_wait(barrier, len(partners))

    for j in (2, 1, 3):
        q = lax.rem(y + j, NY)
        send(a_out.at[q], a_in.at[y], a_sem.at[y], (y_dev(j), pr))
    send(p_out, p_in, p_sem.at[0], (d, mate))
    a_in[y] = a_out[y]

    for q in range(4):
        v = xv[pl.ds(8 * q, 8)]
        w_out[0, pl.ds(8 * q, 8)] = jnp.sum(v * wt_m[None], axis=1)
        w_out[0, pl.ds(32 + 8 * q, 8)] = jnp.sum(v * mt_m[None], axis=1)
        w_out[1, pl.ds(8 * q, 8)] = jnp.sum(v * wh_m[None], axis=1)
        w_out[1, pl.ds(32 + 8 * q, 8)] = jnp.sum(v * mh_m[None], axis=1)
    w_out[0, 64:72] = stack_rows([wl_r, ml_r])
    w_out[1, 64:72] = stack_rows([wf_r, mf_r])
    send(w_out.at[0], w_in.at[0], w_sem.at[0], (after, pr))
    send(w_out.at[1], w_in.at[1], w_sem.at[1], (ahead, pr))

    landed(p_in, p_sem.at[0])
    x_in[xx] = p_out[...] + p_in[...]
    for j in (2, 1, 3):
        send(x_in.at[xx], x_in.at[xx], x_sem.at[xx], (d, x_dev(j)))

    for j in (1, 2, 3):
        i = lax.rem(y + j, NY)
        landed(a_in.at[i], a_sem.at[i])
    tot = [a_in[i, 0:8] for i in range(NY)]
    y_tail = [a_in[i, 8:16] for i in range(NY)]
    y_head = [a_in[i, 16:24] for i in range(NY)]
    first = [a_in[i, 24:25] for i in range(NY)]
    last = [a_in[i, 25:26] for i in range(NY)]
    t_all = (tot[0] + tot[1]) + (tot[2] + tot[3])
    b_out[0, 0:8] = t_all
    b_out[1, 0:8] = t_all
    b_out[0, 8:16] = sum(same(last[i], last[3]) * y_tail[i] for i in range(NY))
    b_out[1, 8:16] = sum(same(first[i], first[0]) * y_head[i] for i in range(NY))
    b_out[0, 16:24] = jnp.broadcast_to(last[3], (8, L))
    b_out[1, 16:24] = jnp.broadcast_to(first[0], (8, L))

    def spread_z(out, inn, sem, rows):
        for k in (4, -4, 3, -3, 2, -2, 1, -1):
            side, n = (0 if k > 0 else 1), rows[abs(k)]
            slot = SLOT[-k]
            send(
                out.at[side, pl.ds(0, n)], inn.at[slot, pl.ds(0, n)], sem.at[slot],
                (z_dev(k), pr),
            )

    def landed_z(inn, sem, rows):
        for o in (1, -1, 2, -2, 3, -3, 4, -4):
            landed(inn.at[SLOT[o], pl.ds(0, rows[abs(o)])], sem.at[SLOT[o]])

    b_rows = {1: 24, 2: 24, 3: 24, 4: 8}
    spread_z(b_out, b_in, b_sem, b_rows)

    for j in (1, 3, 2):
        i = lax.rem(xx + j, NX)
        landed(x_in.at[i], x_sem.at[i])
    day = (x_in[0] + x_in[1]) + (x_in[2] + x_in[3])
    glob[0:SPAN] = day

    def over(m):
        v = day if m is None else day * m
        return jnp.sum(v, axis=0, keepdims=True)

    g_out[0:8] = stack_rows([over(None), over(yt_m), over(yh_m), yf_r, yl_r])
    g_out[8:16] = stack_rows(
        [over(wt_m), over(mt_m), over(wh_m), over(mh_m), wf_r, wl_r, mf_r, ml_r]
    )
    g_in[y] = g_out[...]
    for j in (2, 1, 3):
        send(g_out, g_in.at[y], g_sem.at[y], (y_dev(j), pr))

    landed(w_in.at[0], w_sem.at[0])
    landed(w_in.at[1], w_sem.at[1])
    has_prev, has_next = gate(d > 0), gate(d < NZ * NY - 1)
    carry[WIN] = (has_prev * same(w_in[0, 64:65], wf_r)) * w_in[0, 0:32]
    carry[MIN] = (has_prev * same(w_in[0, 65:66], mf_r)) * w_in[0, 32:64]
    carry[WBK] = (has_next * same(w_in[1, 64:65], wl_r)) * w_in[1, 0:32]
    carry[MBK] = (has_next * same(w_in[1, 65:66], ml_r)) * w_in[1, 32:64]

    for j in (1, 3, 2):
        i = lax.rem(y + j, NY)
        landed(g_in.at[i], g_sem.at[i])
    g_tot = [g_in[i, 0:1] for i in range(NY)]
    g_first = [g_in[i, 3:4] for i in range(NY)]
    g_last = [g_in[i, 4:5] for i in range(NY)]
    g_tail = [g_in[i, 1:2] for i in range(NY)]
    g_head = [g_in[i, 2:3] for i in range(NY)]
    gb_out[0, 0:8] = stack_rows(
        [
            (g_tot[0] + g_tot[1]) + (g_tot[2] + g_tot[3]),
            sum(same(g_last[i], g_last[3]) * g_tail[i] for i in range(NY)),
            sum(same(g_first[i], g_first[0]) * g_head[i] for i in range(NY)),
            g_first[0],
            g_last[3],
        ]
    )
    gb_out[1, 0:8] = gb_out[0, 0:8]
    gb_out[0, 8:16] = g_in[3, 8:16]
    gb_out[1, 8:16] = g_in[0, 8:16]
    g_rows = {1: 16, 2: 8, 3: 8, 4: 8}
    spread_z(gb_out, gb_in, gb_sem, g_rows)

    def earlier(o, to):
        return gate(z_pos(o) < z_pos(to))

    landed_z(b_in, b_sem, b_rows)
    b_tot = {o: b_in[SLOT[o], 0:8] for o in OFFS}
    b2_out[0] = sum(earlier(o, REACH) * b_tot[o] for o in (-4, -3, -2, -1))
    b2_out[1] = sum(earlier(o, -REACH) * b_tot[o] for o in (1, 2, 3))
    send(b2_out.at[0], b2_in.at[0], b2_sem.at[0], (z_dev(REACH), pr))
    send(b2_out.at[1], b2_in.at[1], b2_sem.at[1], (z_dev(-REACH), pr))
    back = [gate(z + o >= 0) for o in (-1, -2, -3)]
    forth = [gate(z + o < NZ) for o in (1, 2, 3)]
    for i in range(NY):
        into = jnp.zeros((8, L), F32)
        out = jnp.zeros((8, L), F32)
        for n, o in enumerate((-1, -2, -3)):
            s = SLOT[o]
            into += (back[n] * same(b_in[s, 16:17], first[i])) * b_in[s, 8:16]
        for e in range(i):
            into += same(last[e], first[i]) * y_tail[e]
        for n, o in enumerate((1, 2, 3)):
            s = SLOT[o]
            out += (forth[n] * same(b_in[s, 16:17], last[i])) * b_in[s, 8:16]
        for e in range(i + 1, NY):
            out += same(first[e], last[i]) * y_head[e]
        c1_out[i, 0:8] = into
        c1_out[i, 8:16] = out
    for j in (2, 1, 3):
        i = lax.rem(y + j, NY)
        send(c1_out.at[i], c1_in.at[y], c1_sem.at[y], (y_dev(j), pr))
    c1_in[y] = c1_out[y]
    direct = sum(earlier(o, 0) * b_tot[o] for o in OFFS)

    landed_z(gb_in, gb_sem, g_rows)
    gb_tot = {o: gb_in[SLOT[o], 0:8] for o in OFFS}
    gb2_out[0] = sum(earlier(o, REACH) * gb_tot[o] for o in (-4, -3, -2, -1))
    gb2_out[1] = sum(earlier(o, -REACH) * gb_tot[o] for o in (1, 2, 3))
    send(gb2_out.at[0], gb2_in.at[0], gb2_sem.at[0], (z_dev(REACH), pr))
    send(gb2_out.at[1], gb2_in.at[1], gb2_sem.at[1], (z_dev(-REACH), pr))
    g_direct = sum(earlier(o, 0) * gb_tot[o] for o in OFFS)

    landed(b2_in.at[0], b2_sem.at[0])
    landed(b2_in.at[1], b2_sem.at[1])
    upto = direct + (b2_in[0] + b2_in[1])
    for i in range(NY):
        c2_out[i] = upto
        upto = upto + tot[i]
    for j in (2, 1, 3):
        i = lax.rem(y + j, NY)
        send(c2_out.at[i], c2_in.at[y], c2_sem.at[y], (y_dev(j), pr))
    c2_in[y] = c2_out[y]

    into = jnp.zeros((1, L), F32)
    out = jnp.zeros((1, L), F32)
    for n, o in enumerate((-1, -2, -3)):
        s = SLOT[o]
        into += (back[n] * same(gb_in[s, 4:5], yf_r)) * gb_in[s, 1:2]
    for n, o in enumerate((1, 2, 3)):
        s = SLOT[o]
        out += (forth[n] * same(gb_in[s, 3:4], yl_r)) * gb_in[s, 2:3]
    within = jnp.zeros((1, L), F32)
    for e in range(NY):
        before, later = gate(y > e), gate(y < e)
        into += (before * same(g_last[e], yf_r)) * g_tail[e]
        out += (later * same(g_first[e], yl_r)) * g_head[e]
        within += before * g_tot[e]
    prev = jnp.where(y > 0, g_in[lax.rem(y + 3, NY), 8:16], gb_in[SLOT[-1], 8:16])
    nxt = jnp.where(y < NY - 1, g_in[lax.rem(y + 1, NY), 8:16], gb_in[SLOT[1], 8:16])
    win = (has_prev * same(prev[5:6], wf_r)) * prev[0:1]
    min_ = (has_prev * same(prev[7:8], mf_r)) * prev[1:2]
    wbk = (has_next * same(nxt[4:5], wl_r)) * nxt[2:3]
    mbk = (has_next * same(nxt[6:7], ml_r)) * nxt[3:4]
    landed(gb2_in.at[0], gb2_sem.at[0])
    landed(gb2_in.at[1], gb2_sem.at[1])
    run = (g_direct + (gb2_in[0] + gb2_in[1]))[0:1] + within
    glob[SPAN:SPAN + 8] = stack_rows([run, win, min_, into, wbk, mbk, out])

    for j in (1, 3, 2):
        i = lax.rem(y + j, NY)
        landed(c1_in.at[i], c1_sem.at[i])
    for q in range(4):
        carry[YIN, pl.ds(8 * q, 8)] = c1_in[q, 0:8]
        carry[YBK, pl.ds(8 * q, 8)] = c1_in[q, 8:16]
    for j in (1, 3, 2):
        i = lax.rem(y + j, NY)
        landed(c2_in.at[i], c2_sem.at[i])
    for q in range(4):
        carry[RUN, pl.ds(8 * q, 8)] = c2_in[q]
    for cp in sends:
        cp.wait_send()


N_SENDS = 3 + 1 + 2 + 3 + 8 + 3 + 8 + 2 + 3 + 2 + 3


def finish(
    wk, mo, yr, x_ref, carry, glob, run_o, week_o, month_o, year_o, roll_o,
    ov, rv, o_sem, r_sem,
):
    outs = (run_o, week_o, month_o, year_o)
    lane = lax.broadcasted_iota(I32, (8, L), 1)
    upon = jnp.bitwise_and(lane, SPAN - 1)

    ids = [spread(r) for r in (wk, mo, yr)]
    rows = []
    date = lax.broadcasted_iota(I32, (SPAN, L), 0)
    rows.append(gate(jnp.broadcast_to(upon[0:1], (SPAN, L)) <= date))
    starts, ends = [], []
    for ref, down in zip((wk, mo, yr), ids):
        across = jnp.full((8, L), ref[0], I32)
        for u in range(1, SPAN):
            across = jnp.where(upon == u, ref[u], across)
        rows.append(gate(jnp.broadcast_to(across[0:1], (SPAN, L)) == down))
        starts.append(gate(down == ref[0]))
        ends.append(gate(down == ref[SPAN - 1]))
    mix = jnp.concatenate(rows, axis=0)[:, 0:3 * SPAN].astype(jnp.bfloat16)

    def sums(v):
        hi = v.astype(jnp.bfloat16)
        rest = v - hi.astype(F32)
        mid = rest.astype(jnp.bfloat16)
        low = (rest - mid.astype(F32)).astype(jnp.bfloat16)
        return jnp.dot(
            mix, jnp.concatenate([hi, mid, low], axis=0), preferred_element_type=F32
        )

    def put(res, row, store):
        store(0, res[0:SPAN] + row(RUN))
        for n in range(3):
            store(
                n + 1,
                res[SPAN * (n + 1):SPAN * (n + 2)]
                + starts[n] * row(WIN + n)
                + ends[n] * row(WBK + n),
            )

    def chunk(c):
        return [
            pltpu.make_async_copy(
                ov.at[k, pl.ds(8 * c, 8)], outs[k].at[pl.ds(8 * c, 8)], o_sem.at[k, c]
            )
            for k in range(4)
        ]

    for c in range(4):
        def body(i, _):
            p = 8 * c + 2 * i
            res = sums(jnp.concatenate([x_ref[p], x_ref[p + 1]], axis=1))
            for h in range(2):
                def store(k, v):
                    ov[k, p + h] = v

                put(
                    res[:, h * L:(h + 1) * L],
                    lambda k: carry[k, pl.ds(p + h, 1)],
                    store,
                )
            return 0

        lax.fori_loop(0, 4, body, 0, unroll=True)
        for cp in chunk(c):
            cp.start()

    res = sums(glob[0:SPAN])

    def store_roll(k, v):
        rv[k] = v

    put(res, lambda k: glob[SPAN + k:SPAN + k + 1], store_roll)
    roll = pltpu.make_async_copy(rv, roll_o, r_sem)
    roll.start()
    for c in range(4):
        for cp in chunk(c):
            cp.wait()
    roll.wait()


def local(daily_sales, week_id, month_id, year_id):
    smem = pl.BlockSpec(memory_space=pltpu.SMEM)
    vmem = pl.BlockSpec(memory_space=pltpu.VMEM)
    hbm = pl.BlockSpec(memory_space=pl.ANY)
    dma = pltpu.SemaphoreType.DMA
    carry, glob = pl.pallas_call(
        exchange,
        name="exchange",
        out_shape=(
            jax.ShapeDtypeStruct((7, COLS, L), F32),
            jax.ShapeDtypeStruct((SPAN + 8, L), F32),
        ),
        in_specs=[smem, smem, smem, hbm],
        out_specs=(vmem, vmem),
        scratch_shapes=[
            pltpu.VMEM((COLS, SPAN, L), F32),
            pltpu.VMEM((NY, 32, L), F32), pltpu.VMEM((NY, 32, L), F32),
            pltpu.VMEM((2, 72, L), F32), pltpu.VMEM((2, 72, L), F32),
            pltpu.VMEM((SPAN, L), F32), pltpu.VMEM((SPAN, L), F32),
            pltpu.VMEM((NX, SPAN, L), F32),
            pltpu.VMEM((2, 24, L), F32), pltpu.VMEM((8, 24, L), F32),
            pltpu.VMEM((2, 8, L), F32), pltpu.VMEM((2, 8, L), F32),
            pltpu.VMEM((NY, 16, L), F32), pltpu.VMEM((NY, 16, L), F32),
            pltpu.VMEM((NY, 8, L), F32), pltpu.VMEM((NY, 8, L), F32),
            pltpu.VMEM((16, L), F32), pltpu.VMEM((NY, 16, L), F32),
            pltpu.VMEM((2, 16, L), F32), pltpu.VMEM((8, 16, L), F32),
            pltpu.VMEM((2, 8, L), F32), pltpu.VMEM((2, 8, L), F32),
            dma((4,)), dma((N_SENDS,)), dma((NY,)), dma((2,)), dma((1,)), dma((NX,)),
            dma((8,)), dma((2,)), dma((NY,)), dma((NY,)),
            dma((NY,)), dma((8,)), dma((2,)),
        ],
        compiler_params=pltpu.CompilerParams(
            collective_id=0, has_side_effects=True, vmem_limit_bytes=8 * 1024 * 1024
        ),
    )(week_id, month_id, year_id, daily_sales)
    big = jax.ShapeDtypeStruct(daily_sales.shape, F32)
    return pl.pallas_call(
        finish,
        name="finish",
        out_shape=(big, big, big, big, jax.ShapeDtypeStruct((4, SPAN, L), F32)),
        in_specs=[smem, smem, smem, vmem, vmem, vmem],
        out_specs=(hbm,) * 5,
        scratch_shapes=[
            pltpu.VMEM((4, COLS, SPAN, L), F32), pltpu.VMEM((4, SPAN, L), F32),
            dma((4, 4)), dma,
        ],
        compiler_params=pltpu.CompilerParams(vmem_limit_bytes=16 * 1024 * 1024),
    )(week_id, month_id, year_id, daily_sales, carry, glob)


def solution(mesh):
    return jax.shard_map(
        local,
        mesh=mesh,
        in_specs=(P("prod", "date", None), P("date"), P("date"), P("date")),
        out_specs=(
            P("prod", "date", None),
            P("prod", "date", None),
            P("prod", "date", None),
            P("prod", "date", None),
            P(None, "date", None),
        ),
        check_vma=False,
    )
```

time: 169 us -> 38.8 us (0.23)
  the two profiles are of different devices: /device:TPU:1 before, /device:TPU:8 now
where the time goes in v1:
time: 38.8 us; the launch traced here: 38.6 us
  Pallas kernels  34.3 us (88%)
  local copies, waits for them, and re-layouts  3.66 us (9%)
  between operations  0.68 us (2%)
    pallas_call x1, Pallas kernels, local(): pl.pallas_call(exchange, name='exchange', out_shape=(jax.ShapeDtypeStruct...  31.9 us
    unnamed x16, local copies, waits for them, and re-layouts  3.66 us
    pallas_call x1, Pallas kernels, local(): pl.pallas_call(finish, name='finish', out_shape=(big, big, big, big, jax....  2.36 us

profile of v1, /device:TPU:8, one launch (start us, length us, event | category | flops | bytes accessed | tf_op | source)
XLA Modules:
  0.0 38.6 jit_solution(13424497359534140204)
XLA Ops:
  0.6 0.0 copy-start
  0.6 1.0 %copy-done = f32[32,32,128]{2,1,0:T(8,128)S(1)} copy-done((f32[32,32,128]{2,1,0:T(8,128)S(1)}, f32[32,32,128]{2,1,0:T(8,128)}, u32[]{:S(2)}) %copy-start) | copy-done | bytes 524312
  1.7 0.0 copy-start.2
  1.7 0.7 %copy-done.2 = s32[32]{0:T(128)S(1)} copy-done((s32[32]{0:T(128)S(1)}, s32[32]{0:T(128)}, u32[]{:S(2)}) %copy-start.2) | copy-done | bytes 152
  2.3 0.0 copy-start.4
  2.3 0.7 %copy-done.4 = s32[32]{0:T(128)S(1)} copy-done((s32[32]{0:T(128)S(1)}, s32[32]{0:T(128)}, u32[]{:S(2)}) %copy-start.4) | copy-done | bytes 152
  3.0 0.0 copy-start.6
  3.0 0.7 %copy-done.6 = s32[32]{0:T(128)S(1)} copy-done((s32[32]{0:T(128)S(1)}, s32[32]{0:T(128)}, u32[]{:S(2)}) %copy-start.6) | copy-done | bytes 152
  3.6 0.0 copy-start.1
  3.6 31.9 %exchange.1 = (f32[7,32,128]{2,1,0:T(8,128)S(1)}, f32[40,128]{1,0:T(8,128)S(1)}) custom-call(s32[32]{0:T(128)S(1)} %copy-done.2, s32[32]{0:T(128)S(1)} %copy-done.4, s32[32]{0:T(128)S(1)} %copy-done.6, f32[32,32,128]{2,1,0:T(8,128)S(1)} %copy-done), custom_call_target="tpu_custom_call" | custom-call | tf_op jit(solution)/shard_map/exchange/pallas_call | solution.py:422
  35.6 0.0 copy-start.3
  35.6 0.0 copy-start.5
  35.6 0.0 copy-start.7
  35.6 0.0 copy-done.1
  35.6 0.6 %copy-done.3 = s32[32]{0:T(128)S(1)} copy-done((s32[32]{0:T(128)S(1)}, s32[32]{0:T(128)}, u32[]{:S(2)}) %copy-start.3) | copy-done | bytes 152
  36.2 0.0 copy-done.5
  36.3 0.0 copy-done.7
  36.3 2.4 %finish.1 = (f32[32,32,128]{2,1,0:T(8,128)}, f32[32,32,128]{2,1,0:T(8,128)}, f32[32,32,128]{2,1,0:T(8,128)}, f32[32,32,128]{2,1,0:T(8,128)}, f32[4,32,128]{2,1,0:T(8,128)}) custom-call(s32[32]{0:T(128)S(1)} %copy-done.3, s32[32]{0:T(128)S(1)} %copy-done.5, s32[32]{0:T(128)S(1)} %copy-done.7, f32[32,32,128]{2,1,0:T(8,128)S(1)} %copy-done.1, ...), custom_call_target="tpu_custom_call" | custom-call | tf_op jit(solution)/shard_map/finish/pallas_call | solution.py:453
Async XLA Ops:
  0.6 1.0 %copy-start = (f32[32,32,128]{2,1,0:T(8,128)S(1)}, f32[32,32,128]{2,1,0:T(8,128)}, u32[]{:S(2)}) copy-start(f32[32,32,128]{2,1,0:T(8,128)} %x_ref.1) | copy-start | bytes 1572868
  1.7 0.7 %copy-start.2 = (s32[32]{0:T(128)S(1)}, s32[32]{0:T(128)}, u32[]{:S(2)}) copy-start(s32[32]{0:T(128)} %wk.3) | copy-start | bytes 388
  2.3 0.7 %copy-start.4 = (s32[32]{0:T(128)S(1)}, s32[32]{0:T(128)}, u32[]{:S(2)}) copy-start(s32[32]{0:T(128)} %mo.3) | copy-start | bytes 388
  3.0 0.7 %copy-start.6 = (s32[32]{0:T(128)S(1)}, s32[32]{0:T(128)}, u32[]{:S(2)}) copy-start(s32[32]{0:T(128)} %yr.3) | copy-start | bytes 388
  3.6 32.0 %copy-start.1 = (f32[32,32,128]{2,1,0:T(8,128)S(1)}, f32[32,32,128]{2,1,0:T(8,128)}, u32[]{:S(2)}) copy-start(f32[32,32,128]{2,1,0:T(8,128)} %x_ref.1) | copy-start | bytes 1572868
  35.6 0.7 %copy-start.3 = (s32[32]{0:T(128)S(1)}, s32[32]{0:T(128)}, u32[]{:S(2)}) copy-start(s32[32]{0:T(128)} %wk.3) | copy-start | bytes 388
  35.6 0.7 %copy-start.5 = (s32[32]{0:T(128)S(1)}, s32[32]{0:T(128)}, u32[]{:S(2)}) copy-start(s32[32]{0:T(128)} %mo.3) | copy-start | bytes 388
  35.6 0.7 %copy-start.7 = (s32[32]{0:T(128)S(1)}, s32[32]{0:T(128)}, u32[]{:S(2)}) copy-start(s32[32]{0:T(128)} %yr.3) | copy-start | bytes 388
